TPU v7x, 32 devices: a whole 2x2x4 slice. The times are simulated.
32 devices in a mesh: row: 8 (over y, x, core), col: 4 (over z).
Axes of the slice: x: 2, y: 2, z: 4, core: 2. Of those that a mesh axis runs over, the one named last changes fastest.
Arguments:
- field: float32 [64, 128, 512], P(None, 'row', 'col'), may hold values from -4 to 6.5, as said below
- conductivity: float32 [64, 128, 512], P(None, 'row', 'col'), may hold values from 35 to 5600, as said below
Outputs:
- new_field: float32 [64, 128, 512], P(None, 'row', 'col')
Inputs may be any that keep to these rules, and one draw needn't show every extreme that they name: `field`: finite values. `conductivity`: positive in every cell.
All inputs are finite; a program needn't handle non-finite values.
Results may differ from a plain program's by a relative error of at most 0.0003.
Values sent between devices are 32-bit elements; how exact they have to be, the bound alone decides.
A program may use at most 64 MiB of HBM per device.

v0:
```python
import jax
import jax.numpy as jnp
from jax import lax
from jax.sharding import PartitionSpec as P

z_weight = 0.02


def padded_2(block, sides, width):
    for axis, dim in sides:
        count = lax.axis_size(axis)
        forward = [(i, i + 1) for i in range(count - 1)]
        backward = [(target, source) for source, target in forward]
        low = lax.ppermute(
            lax.slice_in_dim(block, block.shape[dim] - width, None, axis=dim), axis, forward
        )
        high = lax.ppermute(lax.slice_in_dim(block, 0, width, axis=dim), axis, backward)
        block = jnp.concatenate([low, block, high], axis=dim)
    return block


def neighbour(values, line_axis, offset):
    length = values.shape[line_axis]
    widths = [(0, 0)] * values.ndim
    widths[line_axis] = (1, 1)
    padded = jnp.pad(values, widths)
    return lax.slice_in_dim(padded, 1 + offset, 1 + offset + length, axis=line_axis)


def shifted(values, line_axis, stride, fill):
    length = values.shape[line_axis]
    pad_shape = list(values.shape)
    pad_shape[line_axis] = abs(stride)
    padding = jnp.full(pad_shape, fill, values.dtype)
    if stride > 0:
        kept_part = lax.slice_in_dim(values, 0, length - stride, axis=line_axis)
        return jnp.concatenate((padding, kept_part), axis=line_axis)
    kept_part = lax.slice_in_dim(values, -stride, length, axis=line_axis)
    return jnp.concatenate((kept_part, padding), axis=line_axis)


def reduce_lines(below_diag, diagonal, above_diag, columns, line_axis):
    length = diagonal.shape[line_axis]
    stride = 1
    while stride < length:
        left_factor = -below_diag / shifted(diagonal, line_axis, stride, 1.0)
        right_factor = -above_diag / shifted(diagonal, line_axis, -stride, 1.0)
        new_diag = (
            diagonal
            + left_factor * shifted(above_diag, line_axis, stride, 0.0)
            + right_factor * shifted(below_diag, line_axis, -stride, 0.0)
        )
        new_below = left_factor * shifted(below_diag, line_axis, stride, 0.0)
        new_above = right_factor * shifted(above_diag, line_axis, -stride, 0.0)
        columns = [
            column
            + left_factor * shifted(column, line_axis, stride, 0.0)
            + right_factor * shifted(column, line_axis, -stride, 0.0)
            for column in columns
        ]
        below_diag, diagonal, above_diag = (new_below, new_diag, new_above)
        stride = stride * 2
    return (diagonal, columns)


def local_spikes(below_diag, above_diag, right_side, line_axis):
    length = right_side.shape[line_axis]
    position = lax.broadcasted_iota(jnp.int32, right_side.shape, line_axis)
    first_row = position == 0
    last_row = position == length - 1
    diagonal = 1.0 - below_diag - above_diag
    left_column = jnp.where(first_row, below_diag, 0.0)
    right_column = jnp.where(last_row, above_diag, 0.0)
    below_inner = jnp.where(first_row, 0.0, below_diag)
    above_inner = jnp.where(last_row, 0.0, above_diag)
    diagonal, columns = reduce_lines(
        below_inner, diagonal, above_inner, [right_side, left_column, right_column], line_axis
    )
    local_part = columns[0] / diagonal
    left_spike = columns[1] / diagonal
    right_spike = columns[2] / diagonal
    planes = []
    for member in (local_part, left_spike, right_spike):
        planes.append(lax.index_in_dim(member, 0, line_axis, keepdims=False))
        planes.append(lax.index_in_dim(member, length - 1, line_axis, keepdims=False))
    return (local_part, left_spike, right_spike, jnp.stack(planes)[None])


def join_spikes(gathered, local_part, left_spike, right_spike, line_axis, index_here, group_size):
    columns_in = tuple((gathered[:, member] for member in range(6)))
    zero_plane = jnp.zeros_like(columns_in[0][0])

    def forward(state_now, inputs):
        spike_prev, carry_prev = state_now
        head_local, tail_local, head_left, tail_left, head_right, tail_right = inputs
        pivot_here = 1.0 - head_left * spike_prev
        ratio_here = head_right / pivot_here
        first_here = (head_local - head_left * carry_prev) / pivot_here
        spike_next = tail_right + tail_left * spike_prev * ratio_here
        carry_next = tail_local - tail_left * carry_prev + tail_left * spike_prev * first_here
        return ((spike_next, carry_next), (ratio_here, spike_next, first_here, carry_next))

    unused, outputs = lax.scan(forward, (zero_plane, zero_plane), columns_in)

    def backward(next_head, inputs):
        ratio_here, spike_here, first_here, last_here = inputs
        head_value = first_here - ratio_here * next_head
        tail_value = last_here - spike_here * next_head
        return (head_value, (head_value, tail_value))

    unused_last, ends = lax.scan(backward, zero_plane, outputs, reverse=True)
    first_values, last_values = ends
    left_value = lax.dynamic_index_in_dim(
        last_values, jnp.maximum(index_here - 1, 0), 0, keepdims=False
    ) * (index_here > 0).astype(jnp.float32)
    right_value = lax.dynamic_index_in_dim(
        first_values, jnp.minimum(index_here + 1, group_size - 1), 0, keepdims=False
    ) * (index_here < group_size - 1).astype(jnp.float32)
    return (
        local_part
        - jnp.expand_dims(left_value, line_axis) * left_spike
        - jnp.expand_dims(right_value, line_axis) * right_spike
    )


def on_device(field, conductivity):
    stacked = jnp.stack((field, conductivity))
    padded = padded_2(stacked, (("row", 2), ("col", 3)), 1)
    field_pad = padded[0]
    cond_pad = padded[1]
    west_cond = cond_pad[:, :-2, 1:-1]
    east_cond = cond_pad[:, 2:, 1:-1]
    south_cond = cond_pad[:, 1:-1, :-2]
    north_cond = cond_pad[:, 1:-1, 2:]
    west_field = field_pad[:, :-2, 1:-1]
    east_field = field_pad[:, 2:, 1:-1]
    south_field = field_pad[:, 1:-1, :-2]
    north_field = field_pad[:, 1:-1, 2:]
    east_xdir = 0.5 * 1.0 * (conductivity + east_cond)
    west_xdir = 0.5 * 1.0 * (conductivity + west_cond)
    east_ydir = 0.5 * 1.0 * (conductivity + north_cond)
    west_ydir = 0.5 * 1.0 * (conductivity + south_cond)
    flux_xdir = east_xdir * (east_field - field) - west_xdir * (field - west_field)
    flux_ydir = east_ydir * (north_field - field) - west_ydir * (field - south_field)
    east_zdir = 0.5 * z_weight * (conductivity + neighbour(conductivity, 0, 1))
    west_zdir = 0.5 * z_weight * (conductivity + neighbour(conductivity, 0, -1))
    flux_zdir = east_zdir * (neighbour(field, 0, 1) - field) - west_zdir * (
        field - neighbour(field, 0, -1)
    )
    explicit = flux_xdir + flux_ydir + flux_zdir
    local_part, left_spike, right_spike, planes = local_spikes(-west_xdir, -east_xdir, explicit, 1)
    gathered = lax.all_gather(planes, "row", axis=0, tiled=True)
    delta_xdir = join_spikes(
        gathered,
        local_part,
        left_spike,
        right_spike,
        1,
        lax.axis_index("row"),
        lax.axis_size("row"),
    )
    local_part, left_spike, right_spike, planes = local_spikes(
        -west_ydir, -east_ydir, delta_xdir, 2
    )
    gathered = lax.all_gather(planes, "col", axis=0, tiled=True)
    delta_ydir = join_spikes(
        gathered,
        local_part,
        left_spike,
        right_spike,
        2,
        lax.axis_index("col"),
        lax.axis_size("col"),
    )
    return field + delta_ydir


def solution(mesh):
    in_specs = (P(None, "row", "col"), P(None, "row", "col"))
    out_specs = P(None, "row", "col")
    return jax.shard_map(
        on_device, mesh=mesh, in_specs=in_specs, out_specs=out_specs, check_vma=False
    )
```

profile of v0, /device:TPU:0, one launch (start us, length us, event | category | flops | bytes accessed | tf_op | source)
XLA Modules:
  0.0 144.2 jit_solution(15308119017377806291)
XLA Ops:
  6.5 2.5 %fusion.59 = (f32[64,16,128]{2,0,1:T(8,128)}, f32[1,64,16,128]{3,1,2,0:T(8,128)S(1)}, f32[1,64,16,128]{3,1,2,0:T(8,128)S(1)}, f32[64,16,128]{2,0,1:T(8,128)}) fusion(f32[64,16,128]{2,1,0:T(8,128)} %param.10, f32[64,16,128]{2,1,0:T(8,128)} %param.11), kind=kLoop, calls=%fused_computation.241 | loop fusion | bytes 3145728 | tf_op args[0]
  9.1 1.3 collective-permute-start.1
  10.4 3.0 %collective-permute-start = (f32[2,64,1,128]{3,1,2,0:T(8,128)S(1)}, f32[2,64,1,128]{3,1,2,0:T(8,128)S(1)}, u32[]{:S(2)}, u32[]{:S(2)}) collective-permute-start(f32[2,64,1,128]{3,1,2,0:T(8,128)S(1)} %get-tuple-element.850), channel_id=1, source_target_pairs={{0,4},{4,8},{8,12},{12,16},{16,20},{20,24},{24,28},{1,5},{5,9},{9,... | collective-permute-start | bytes 196616 | tf_op jit(solution)/shard_map/ppermute | solution.py:14
  13.4 0.9 collective-permute-done
  14.9 1.0 copy.304
  15.9 1.3 collective-permute-start.3
  17.6 6.2 %collective-permute-start.2 = (f32[2,64,18,1]{1,0,3,2:T(2,128)S(1)}, f32[2,64,18,1]{1,0,3,2:T(2,128)}, u32[]{:S(2)}, u32[]{:S(2)}) collective-permute-start(f32[2,64,18,1]{1,0,3,2:T(2,128)S(1)} %copy.303), channel_id=1, source_target_pairs={{0,1},{1,2},{2,3},{4,5},{5,6},{6,7},{8,9},{9,10},{10,11},{12,13},{... | collective-permute-start | bytes 27656 | tf_op jit(solution)/shard_map/ppermute | solution.py:14
  24.6 1.1 copy.305
  25.8 1.0 pad_maximum_fusion
  27.0 0.8 copy-done
  28.1 1.1 subtract_subtract_fusion.1
  29.5 0.8 multiply_add_fusion.30
  31.0 1.0 multiply_add_fusion.37
  32.8 0.8 multiply_add_fusion.35
  34.0 0.7 multiply_add_fusion.33
  36.0 0.8 copy-done.8
  37.0 0.7 copy-done.21
  38.2 0.8 copy-done.1
  39.1 0.7 multiply_add_fusion.11
  39.8 1.3 fusion.87
  41.1 1.2 fusion.107
  42.3 1.0 fusion.106
  43.2 1.1 fusion.104
  44.6 1.2 fusion.105
  45.8 23.3 %all-gather.4.cloned.1.call-done = f32[48,64,128]{2,1,0:T(8,128)} async-done(((f32[6,64,128]{2,1,0:T(8,128)}), f32[48,64,128]{2,1,0:T(8,128)}) %all-gather.4.cloned.1.call-update) | async-done | bytes 1572880 | tf_op jit(solution)/shard_map/all_gather | solution.py:152
  69.1 2.4 %slice_bitcast_fusion.2 = (f32[8,64,128]{2,1,0:T(8,128)S(1)}, f32[8,64,128]{2,1,0:T(8,128)S(1)}, f32[8,64,128]{2,1,0:T(8,128)}, f32[8,64,128]{2,1,0:T(8,128)}, f32[8,64,128]{2,1,0:T(8,128)}, /*index=5*/f32[8,64,128]{2,1,0:T(8,128)}) fusion(f32[8,6,64,128]{3,2,1,0:T(8,128)} %bitcast.281), kind=kLoop, calls=%fused_computation.177 | loop fusion | bytes 3145728 | tf_op jit(solution)/shard_map/squeeze | solution.py:90
  71.5 0.7 broadcast.344.clone.1
  72.2 0.7 broadcast.344.clone.2
  72.9 0.7 broadcast.344.clone.3
  73.7 0.7 broadcast.344.clone.4
  74.4 12.1 %while.80 = (s32[]{:T(128)}, f32[64,128]{1,0:T(8,128)S(1)}, f32[64,128]{1,0:T(8,128)S(1)}, f32[8,64,128]{2,1,0:T(8,128)}, f32[8,64,128]{2,1,0:T(8,128)}, /*index...) while((s32[]{:T(128)}, f32[64,128]{1,0:T(8,128)S(1)}, ...), condition=%wide.region_1.2_spmd.clone, body=%wide.region_0.1_spmd.clone.sunk | while | flops 122883 | bytes 458915 | solution.py:103
  74.4 1.6 %bitcast_dynamic-update-slice_fusion.16 = (f32[8,64,128]{2,1,0:T(8,128)}, f32[64,128]{1,0:T(8,128)S(1)}, f32[8,64,128]{2,1,0:T(8,128)}, f32[8,64,128]{2,1,0:T(8,...) fusion(f32[8,64,128]{2,1,0:T(8,128)} %get-tuple-element.1309, s32[]{:T(128)S(6)} %copy.408, ...), kind=kLoop, calls=%fused_computation.clone.1 | loop fusion | flops 122880 | bytes 458757 | tf_op jit(solution)/shard_map/while/body/jit(dynamic_update_index_in_dim)/dynamic_update_slice | solution.py:103
  76.0 1.5 %bitcast_dynamic-update-slice_fusion.16 = (f32[8,64,128]{2,1,0:T(8,128)}, f32[64,128]{1,0:T(8,128)S(1)}, f32[8,64,128]{2,1,0:T(8,128)}, f32[8,64,128]{2,1,0:T(8,...) fusion(f32[8,64,128]{2,1,0:T(8,128)} %get-tuple-element.1309, s32[]{:T(128)S(6)} %copy.408, ...), kind=kLoop, calls=%fused_computation.clone.1 | loop fusion | flops 122880 | bytes 458757 | tf_op jit(solution)/shard_map/while/body/jit(dynamic_update_index_in_dim)/dynamic_update_slice | solution.py:103
  77.5 1.5 %bitcast_dynamic-update-slice_fusion.16 = (f32[8,64,128]{2,1,0:T(8,128)}, f32[64,128]{1,0:T(8,128)S(1)}, f32[8,64,128]{2,1,0:T(8,128)}, f32[8,64,128]{2,1,0:T(8,...) fusion(f32[8,64,128]{2,1,0:T(8,128)} %get-tuple-element.1309, s32[]{:T(128)S(6)} %copy.408, ...), kind=kLoop, calls=%fused_computation.clone.1 | loop fusion | flops 122880 | bytes 458757 | tf_op jit(solution)/shard_map/while/body/jit(dynamic_update_index_in_dim)/dynamic_update_slice | solution.py:103
  79.0 1.5 %bitcast_dynamic-update-slice_fusion.16 = (f32[8,64,128]{2,1,0:T(8,128)}, f32[64,128]{1,0:T(8,128)S(1)}, f32[8,64,128]{2,1,0:T(8,128)}, f32[8,64,128]{2,1,0:T(8,...) fusion(f32[8,64,128]{2,1,0:T(8,128)} %get-tuple-element.1309, s32[]{:T(128)S(6)} %copy.408, ...), kind=kLoop, calls=%fused_computation.clone.1 | loop fusion | flops 122880 | bytes 458757 | tf_op jit(solution)/shard_map/while/body/jit(dynamic_update_index_in_dim)/dynamic_update_slice | solution.py:103
  80.5 1.5 %bitcast_dynamic-update-slice_fusion.16 = (f32[8,64,128]{2,1,0:T(8,128)}, f32[64,128]{1,0:T(8,128)S(1)}, f32[8,64,128]{2,1,0:T(8,128)}, f32[8,64,128]{2,1,0:T(8,...) fusion(f32[8,64,128]{2,1,0:T(8,128)} %get-tuple-element.1309, s32[]{:T(128)S(6)} %copy.408, ...), kind=kLoop, calls=%fused_computation.clone.1 | loop fusion | flops 122880 | bytes 458757 | tf_op jit(solution)/shard_map/while/body/jit(dynamic_update_index_in_dim)/dynamic_update_slice | solution.py:103
  82.0 1.5 %bitcast_dynamic-update-slice_fusion.16 = (f32[8,64,128]{2,1,0:T(8,128)}, f32[64,128]{1,0:T(8,128)S(1)}, f32[8,64,128]{2,1,0:T(8,128)}, f32[8,64,128]{2,1,0:T(8,...) fusion(f32[8,64,128]{2,1,0:T(8,128)} %get-tuple-element.1309, s32[]{:T(128)S(6)} %copy.408, ...), kind=kLoop, calls=%fused_computation.clone.1 | loop fusion | flops 122880 | bytes 458757 | tf_op jit(solution)/shard_map/while/body/jit(dynamic_update_index_in_dim)/dynamic_update_slice | solution.py:103
  83.5 1.5 %bitcast_dynamic-update-slice_fusion.16 = (f32[8,64,128]{2,1,0:T(8,128)}, f32[64,128]{1,0:T(8,128)S(1)}, f32[8,64,128]{2,1,0:T(8,128)}, f32[8,64,128]{2,1,0:T(8,...) fusion(f32[8,64,128]{2,1,0:T(8,128)} %get-tuple-element.1309, s32[]{:T(128)S(6)} %copy.408, ...), kind=kLoop, calls=%fused_computation.clone.1 | loop fusion | flops 122880 | bytes 458757 | tf_op jit(solution)/shard_map/while/body/jit(dynamic_update_index_in_dim)/dynamic_update_slice | solution.py:103
  85.0 1.5 %bitcast_dynamic-update-slice_fusion.16 = (f32[8,64,128]{2,1,0:T(8,128)}, f32[64,128]{1,0:T(8,128)S(1)}, f32[8,64,128]{2,1,0:T(8,128)}, f32[8,64,128]{2,1,0:T(8,...) fusion(f32[8,64,128]{2,1,0:T(8,128)} %get-tuple-element.1309, s32[]{:T(128)S(6)} %copy.408, ...), kind=kLoop, calls=%fused_computation.clone.1 | loop fusion | flops 122880 | bytes 458757 | tf_op jit(solution)/shard_map/while/body/jit(dynamic_update_index_in_dim)/dynamic_update_slice | solution.py:103
  86.5 0.7 broadcast.344
  87.2 0.7 broadcast.344.clone
  87.9 11.6 %while.81 = (s32[]{:T(128)}, f32[64,128]{1,0:T(8,128)S(1)}, f32[8,64,128]{2,1,0:T(8,128)}, f32[8,64,128]{2,1,0:T(8,128)}, f32[8,64,128]{2,1,0:T(8,128)}, /*index...) while((s32[]{:T(128)}, f32[64,128]{1,0:T(8,128)S(1)}, ...), condition=%wide.region_3.4_spmd.clone, body=%wide.region_2.3_spmd.clone.sunk | while | flops 40964 | bytes 262287 | solution.py:111
  87.9 1.5 %bitcast_dynamic-update-slice_fusion.17 = (f32[8,64,128]{2,1,0:T(8,128)}, f32[64,128]{1,0:T(8,128)S(1)}, f32[8,64,128]{2,1,0:T(8,128)}) fusion(f32[8,64,128]{2,1,0:T(8,128)} %get-tuple-element.1346, s32[]{:T(128)S(6)} %sub.273, f32[64,128]{1,0:T(8,128)S(1)} %get-tuple-element.1345, pred[]{:T(512)S(6)} %compare.143, ...), kind=kLoop, calls=%fused_computation.18.clone.1 | loop fusion | flops 40960 | bytes 262149 | tf_op jit(solution)/shard_map/while/body/jit(dynamic_update_index_in_dim)/dynamic_update_slice | solution.py:103
  89.4 1.4 bitcast_dynamic-update-slice_fusion.17
  90.8 1.5 %bitcast_dynamic-update-slice_fusion.17 = (f32[8,64,128]{2,1,0:T(8,128)}, f32[64,128]{1,0:T(8,128)S(1)}, f32[8,64,128]{2,1,0:T(8,128)}) fusion(f32[8,64,128]{2,1,0:T(8,128)} %get-tuple-element.1346, s32[]{:T(128)S(6)} %sub.273, f32[64,128]{1,0:T(8,128)S(1)} %get-tuple-element.1345, pred[]{:T(512)S(6)} %compare.143, ...), kind=kLoop, calls=%fused_computation.18.clone.1 | loop fusion | flops 40960 | bytes 262149 | tf_op jit(solution)/shard_map/while/body/jit(dynamic_update_index_in_dim)/dynamic_update_slice | solution.py:103
  92.3 1.4 %bitcast_dynamic-update-slice_fusion.17 = (f32[8,64,128]{2,1,0:T(8,128)}, f32[64,128]{1,0:T(8,128)S(1)}, f32[8,64,128]{2,1,0:T(8,128)}) fusion(f32[8,64,128]{2,1,0:T(8,128)} %get-tuple-element.1346, s32[]{:T(128)S(6)} %sub.273, f32[64,128]{1,0:T(8,128)S(1)} %get-tuple-element.1345, pred[]{:T(512)S(6)} %compare.143, ...), kind=kLoop, calls=%fused_computation.18.clone.1 | loop fusion | flops 40960 | bytes 262149 | tf_op jit(solution)/shard_map/while/body/jit(dynamic_update_index_in_dim)/dynamic_update_slice | solution.py:103
  93.7 1.4 %bitcast_dynamic-update-slice_fusion.17 = (f32[8,64,128]{2,1,0:T(8,128)}, f32[64,128]{1,0:T(8,128)S(1)}, f32[8,64,128]{2,1,0:T(8,128)}) fusion(f32[8,64,128]{2,1,0:T(8,128)} %get-tuple-element.1346, s32[]{:T(128)S(6)} %sub.273, f32[64,128]{1,0:T(8,128)S(1)} %get-tuple-element.1345, pred[]{:T(512)S(6)} %compare.143, ...), kind=kLoop, calls=%fused_computation.18.clone.1 | loop fusion | flops 40960 | bytes 262149 | tf_op jit(solution)/shard_map/while/body/jit(dynamic_update_index_in_dim)/dynamic_update_slice | solution.py:103
  95.2 1.5 %bitcast_dynamic-update-slice_fusion.17 = (f32[8,64,128]{2,1,0:T(8,128)}, f32[64,128]{1,0:T(8,128)S(1)}, f32[8,64,128]{2,1,0:T(8,128)}) fusion(f32[8,64,128]{2,1,0:T(8,128)} %get-tuple-element.1346, s32[]{:T(128)S(6)} %sub.273, f32[64,128]{1,0:T(8,128)S(1)} %get-tuple-element.1345, pred[]{:T(512)S(6)} %compare.143, ...), kind=kLoop, calls=%fused_computation.18.clone.1 | loop fusion | flops 40960 | bytes 262149 | tf_op jit(solution)/shard_map/while/body/jit(dynamic_update_index_in_dim)/dynamic_update_slice | solution.py:103
  96.6 1.4 %bitcast_dynamic-update-slice_fusion.17 = (f32[8,64,128]{2,1,0:T(8,128)}, f32[64,128]{1,0:T(8,128)S(1)}, f32[8,64,128]{2,1,0:T(8,128)}) fusion(f32[8,64,128]{2,1,0:T(8,128)} %get-tuple-element.1346, s32[]{:T(128)S(6)} %sub.273, f32[64,128]{1,0:T(8,128)S(1)} %get-tuple-element.1345, pred[]{:T(512)S(6)} %compare.143, ...), kind=kLoop, calls=%fused_computation.18.clone.1 | loop fusion | flops 40960 | bytes 262149 | tf_op jit(solution)/shard_map/while/body/jit(dynamic_update_index_in_dim)/dynamic_update_slice | solution.py:103
  98.1 1.5 %bitcast_dynamic-update-slice_fusion.17 = (f32[8,64,128]{2,1,0:T(8,128)}, f32[64,128]{1,0:T(8,128)S(1)}, f32[8,64,128]{2,1,0:T(8,128)}) fusion(f32[8,64,128]{2,1,0:T(8,128)} %get-tuple-element.1346, s32[]{:T(128)S(6)} %sub.273, f32[64,128]{1,0:T(8,128)S(1)} %get-tuple-element.1345, pred[]{:T(512)S(6)} %compare.143, ...), kind=kLoop, calls=%fused_computation.18.clone.1 | loop fusion | flops 40960 | bytes 262149 | tf_op jit(solution)/shard_map/while/body/jit(dynamic_update_index_in_dim)/dynamic_update_slice | solution.py:103
  99.5 0.8 multiply_bitcast_fusion
  100.3 0.8 multiply_bitcast_fusion.1
  101.5 0.6 copy-done.15
  103.3 2.1 %multiply_add_fusion.24 = (f32[64,16,128]{2,0,1:T(8,128)S(1)}, f32[64,16,128]{2,0,1:T(8,128)S(1)}, f32[64,16,128]{2,0,1:T(8,128)S(1)}, f32[64,16,128]{2,0,1:T(8,...) fusion(f32[64,16,128]{2,0,1:T(8,128)S(1)} %copy-done.5, ...), kind=kLoop, calls=%fused_computation.141 | loop fusion | flops 2359296 | bytes 11476992 | tf_op jit(solution)/shard_map/add | solution.py:56
  106.9 1.0 multiply_add_fusion.22
  109.5 1.0 multiply_add_fusion.20
  112.1 1.0 multiply_add_fusion.18
  114.7 1.0 multiply_add_fusion.16
  116.7 0.7 multiply_add_fusion.14
  118.2 0.8 add_divide_fusion.2
  119.6 0.8 add_divide_fusion.1
  120.4 0.5 slice_reduce_fusion.2
  121.5 13.8 %all-gather.1 = f32[24,64,16]{1,2,0:T(8,128)S(1)} all-gather(f32[6,64,16]{1,2,0:T(8,128)S(1)} %constant_dynamic-update-slice_fusion), channel_id=3, replica_groups=mesh['row'=8,'col'=4] {'col'}, dimensions={0}, use_global_device_ids=true | all-gather | bytes 122880 | tf_op jit(solution)/shard_map/all_gather | solution.py:165
  136.2 1.1 copy.334
  (162 shorter events, 18.3 us)
Async XLA Ops:
  6.5 62.6 %all-gather.4.cloned.1.call-start = ((), (), s32[]{:S(2)}) async-start(), calls=%async_computation | async-start | bytes 1769472 | tf_op jit(solution)/shard_map/all_gather | solution.py:152
  9.1 4.4 %collective-permute-start.1 = (f32[2,64,1,128]{3,1,2,0:T(8,128)S(1)}, f32[2,64,1,128]{3,1,2,0:T(8,128)S(1)}, u32[]{:S(2)}, u32[]{:S(2)}) collective-permute-start(f32[2,64,1,128]{3,1,2,0:T(8,128)S(1)} %get-tuple-element.851), channel_id=1, source_target_pairs={{4,0},{8,4},{12,8},{16,12},{20,16},{24,20},{28,24},{5,1},{9,5},{13... | collective-permute-start | bytes 196616 | tf_op jit(solution)/shard_map/ppermute | solution.py:17
  10.4 3.9 %collective-permute-start = (f32[2,64,1,128]{3,1,2,0:T(8,128)S(1)}, f32[2,64,1,128]{3,1,2,0:T(8,128)S(1)}, u32[]{:S(2)}, u32[]{:S(2)}) collective-permute-start(f32[2,64,1,128]{3,1,2,0:T(8,128)S(1)} %get-tuple-element.850), channel_id=1, source_target_pairs={{0,4},{4,8},{8,12},{12,16},{16,20},{20,24},{24,28},{1,5},{5,9},{9,... | collective-permute-start | bytes 196616 | tf_op jit(solution)/shard_map/ppermute | solution.py:14
  15.9 7.9 %collective-permute-start.3 = (f32[2,64,18,1]{1,0,3,2:T(2,128)}, f32[2,64,18,1]{1,0,3,2:T(2,128)S(1)}, u32[]{:S(2)}, u32[]{:S(2)}) collective-permute-start(f32[2,64,18,1]{1,0,3,2:T(2,128)} %copy.304), channel_id=1, source_target_pairs={{1,0},{2,1},{3,2},{5,4},{6,5},{7,6},{9,8},{10,9},{11,10},{13,12},{... | collective-permute-start | bytes 27656 | tf_op jit(solution)/shard_map/ppermute | solution.py:17
  17.6 7.0 %collective-permute-start.2 = (f32[2,64,18,1]{1,0,3,2:T(2,128)S(1)}, f32[2,64,18,1]{1,0,3,2:T(2,128)}, u32[]{:S(2)}, u32[]{:S(2)}) collective-permute-start(f32[2,64,18,1]{1,0,3,2:T(2,128)S(1)} %copy.303), channel_id=1, source_target_pairs={{0,1},{1,2},{2,3},{4,5},{5,6},{6,7},{8,9},{9,10},{10,11},{12,13},{... | collective-permute-start | bytes 27656 | tf_op jit(solution)/shard_map/ppermute | solution.py:14
  26.8 1.0 copy-start
  26.8 1.2 copy-start.19
  26.8 1.3 copy-start.20
  35.2 0.8 copy-start.6
  36.0 0.8 copy-start.8
  36.0 1.0 copy-start.10
  37.0 0.7 copy-start.21
  38.0 1.0 copy-start.1
  39.8 4.5 %copy-start.2 = (f32[64,16,128]{2,0,1:T(8,128)}, f32[64,16,128]{2,0,1:T(8,128)S(1)}, u32[]{:S(2)}) copy-start(f32[64,16,128]{2,0,1:T(8,128)S(1)} %get-tuple-element.745) | copy-start | bytes 1572868
  39.8 4.5 %copy-start.4 = (f32[64,16,128]{2,0,1:T(8,128)}, f32[64,16,128]{2,0,1:T(8,128)S(1)}, u32[]{:S(2)}) copy-start(f32[64,16,128]{2,0,1:T(8,128)S(1)} %get-tuple-element.747) | copy-start | bytes 1572868
  73.7 27.4 %copy-start.11 = (f32[64,16,128]{2,0,1:T(8,128)S(1)}, f32[64,16,128]{2,0,1:T(8,128)}, u32[]{:S(2)}) copy-start(f32[64,16,128]{2,0,1:T(8,128)} %copy-done.10) | copy-start | bytes 1572868
  74.4 26.7 %copy-start.9 = (f32[64,16,128]{2,0,1:T(8,128)S(1)}, f32[64,16,128]{2,0,1:T(8,128)}, u32[]{:S(2)}) copy-start(f32[64,16,128]{2,0,1:T(8,128)} %copy-done.8) | copy-start | bytes 1572868
  86.5 14.6 %copy-start.7 = (f32[64,16,128]{2,0,1:T(8,128)S(1)}, f32[64,16,128]{2,0,1:T(8,128)}, u32[]{:S(2)}) copy-start(f32[64,16,128]{2,0,1:T(8,128)} %copy-done.6) | copy-start | bytes 1572868
  101.1 1.0 copy-start.15
  101.1 1.2 copy-start.16
  101.1 1.3 copy-start.17
  101.1 1.5 %copy-start.18 = (f32[64,16,127]{2,0,1:T(8,128)S(1)}, f32[64,16,127]{2,0,1:T(8,128)}, u32[]{:S(2)}) copy-start(f32[64,16,127]{2,0,1:T(8,128)} %get-tuple-element.972) | copy-start | bytes 1560580
  101.2 1.5 %copy-start.3 = (f32[64,16,128]{2,0,1:T(8,128)S(1)}, f32[64,16,128]{2,0,1:T(8,128)}, u32[]{:S(2)}) copy-start(f32[64,16,128]{2,0,1:T(8,128)} %copy-done.2) | copy-start | bytes 1572868
  101.2 1.7 %copy-start.5 = (f32[64,16,128]{2,0,1:T(8,128)S(1)}, f32[64,16,128]{2,0,1:T(8,128)}, u32[]{:S(2)}) copy-start(f32[64,16,128]{2,0,1:T(8,128)} %copy-done.4) | copy-start | bytes 1572868
  101.3 1.8 %copy-start.13 = (f32[64,16,127]{2,0,1:T(8,128)S(1)}, f32[64,16,127]{2,0,1:T(8,128)}, u32[]{:S(2)}) copy-start(f32[64,16,127]{2,0,1:T(8,128)} %get-tuple-element.938) | copy-start | bytes 1560580
  101.3 2.0 %copy-start.14 = (f32[64,16,127]{2,0,1:T(8,128)S(1)}, f32[64,16,127]{2,0,1:T(8,128)}, u32[]{:S(2)}) copy-start(f32[64,16,127]{2,0,1:T(8,128)} %get-tuple-element.939) | copy-start | bytes 1560580
  121.5 14.4 %copy-start.12 = (f32[64,16,128]{2,1,0:T(8,128)S(1)}, f32[64,16,128]{2,1,0:T(8,128)}, u32[]{:S(2)}) copy-start(f32[64,16,128]{2,1,0:T(8,128)} %param.10) | copy-start | bytes 1572868
Sparse Core Ops, SparseCore 0:
  37.9 31.1 all-gather.3
where the time goes:
time: 146 us; the launch traced here: 144 us
  other arithmetic  43.1 us (30%)
  local copies, waits for them, and re-layouts  36.4 us (25%)
  waiting for transfers between devices  24.6 us (17%)
  between operations  14.2 us (10%)
  blocking collectives  13.8 us (9%)
  starting transfers between devices  11.8 us (8%)
    dynamic_update_slice x24, other arithmetic, join_spikes(): unused, outputs = lax.scan(forward, (zero_plane, zero_plane), columns_in)  23.8 us
    all_gather x1, waiting for transfers between devices, on_device(): gathered = lax.all_gather(planes, 'row', axis=0, tiled=True)  23.3 us
    all_gather x1, blocking collectives, on_device(): gathered = lax.all_gather(planes, 'col', axis=0, tiled=True)  13.8 us
    add x11, other arithmetic, reduce_lines(): column + left_factor * shifted(column, line_axis, stride, 0.0)  10.7 us
    slice x41, local copies, waits for them, and re-layouts, shifted(): kept_part = lax.slice_in_dim(values, 0, length - stride, axis=line_axis)  9.44 us
    ppermute x2, starting transfers between devices, padded_2(): lax.ppermute(lax.slice_in_dim(block, block.shape[dim] - width, None, axis...  9.22 us
    unnamed x55, local copies, waits for them, and re-layouts  8.25 us
    slice x24, local copies, waits for them, and re-layouts, shifted(): kept_part = lax.slice_in_dim(values, -stride, length, axis=line_axis)  5.6 us
  transfers between devices with their start and end apart: 5, of which 3 were waited for; matrix products, arithmetic and copies ran while one was open for 6% of the time, Pallas kernels for 0%

commit v1 on v0

--- a/solution.py
+++ b/solution.py
@@ -149,7 +149,12 @@
     )
     explicit = flux_xdir + flux_ydir + flux_zdir
     local_part, left_spike, right_spike, planes = local_spikes(-west_xdir, -east_xdir, explicit, 1)
-    gathered = lax.all_gather(planes, "row", axis=0, tiled=True)
+    ring = [planes]
+    for hop in range(7):
+        ring.append(lax.ppermute(ring[-1], "row", [(dev, (dev + 1) % 8) for dev in range(8)]))
+    gathered = jnp.roll(
+        jnp.concatenate(ring[::-1], axis=0), (lax.axis_index("row") + 1) * ring[0].shape[0], axis=0
+    )
     delta_xdir = join_spikes(
         gathered,
         local_part,

time: 146 us -> 143 us (0.979)
  the two profiles are of different devices: /device:TPU:0 before, /device:TPU:4 now
where the time goes in v1:
time: 143 us; the launch traced here: 142 us
  other arithmetic  44.7 us (31%)
  waiting for transfers between devices  38.7 us (27%)
  local copies, waits for them, and re-layouts  31.2 us (22%)
  blocking collectives  14.8 us (10%)
  starting transfers between devices  11.2 us (8%)
    ppermute x7, waiting for transfers between devices, on_device(): lax.ppermute(ring[-1], 'row', [(dev, (dev + 1) % 8) for dev in range(8)])  34.7 us
    dynamic_update_slice x24, other arithmetic, join_spikes(): unused, outputs = lax.scan(forward, (zero_plane, zero_plane), columns_in)  23.6 us
    all_gather x1, blocking collectives, on_device(): gathered = lax.all_gather(planes, 'col', axis=0, tiled=True)  14.8 us
    add x11, other arithmetic, reduce_lines(): column + left_factor * shifted(column, line_axis, stride, 0.0)  9.65 us
    slice x41, local copies, waits for them, and re-layouts, shifted(): kept_part = lax.slice_in_dim(values, 0, length - stride, axis=line_axis)  9.16 us
    ppermute x2, starting transfers between devices, padded_2(): lax.ppermute(lax.slice_in_dim(block, block.shape[dim] - width, None, axis...  7.07 us
    unnamed x64, local copies, waits for them, and re-layouts  5.92 us
    slice x24, local copies, waits for them, and re-layouts, shifted(): kept_part = lax.slice_in_dim(values, -stride, length, axis=line_axis)  5.56 us
  transfers between devices with their start and end apart: 11, of which 8 were waited for; matrix products, arithmetic and copies ran while one was open for 6% of the time, Pallas kernels for 0%

profile of v1, /device:TPU:4, one launch (start us, length us, event | category | flops | bytes accessed | tf_op | source)
XLA Modules:
  0.0 141.8 jit_solution(13421077320948822271)
XLA Ops:
  0.0 2.5 %fusion.53 = (f32[64,16,128]{2,0,1:T(8,128)}, f32[1,64,16,128]{3,1,2,0:T(8,128)S(1)}, f32[1,64,16,128]{3,1,2,0:T(8,128)S(1)}, f32[64,16,128]{2,0,1:T(8,128)}) fusion(f32[64,16,128]{2,1,0:T(8,128)} %param.10, f32[64,16,128]{2,1,0:T(8,128)} %param.11), kind=kLoop, calls=%fused_computation.257 | loop fusion | bytes 3145728 | tf_op args[0]
  2.5 2.8 %collective-permute-start.1 = (f32[2,64,1,128]{3,1,2,0:T(8,128)S(1)}, f32[2,64,1,128]{3,1,2,0:T(8,128)S(1)}, u32[]{:S(2)}, u32[]{:S(2)}) collective-permute-start(f32[2,64,1,128]{3,1,2,0:T(8,128)S(1)} %get-tuple-element.864), channel_id=1, source_target_pairs={{4,0},{8,4},{12,8},{16,12},{20,16},{24,20},{28,24},{5,1},{9,5},{13... | collective-permute-start | bytes 196616 | tf_op jit(solution)/shard_map/ppermute | solution.py:17
  5.3 1.9 %collective-permute-start = (f32[2,64,1,128]{3,1,2,0:T(8,128)S(1)}, f32[2,64,1,128]{3,1,2,0:T(8,128)S(1)}, u32[]{:S(2)}, u32[]{:S(2)}) collective-permute-start(f32[2,64,1,128]{3,1,2,0:T(8,128)S(1)} %get-tuple-element.863), channel_id=1, source_target_pairs={{0,4},{4,8},{8,12},{12,16},{16,20},{20,24},{24,28},{1,5},{5,9},{9,... | collective-permute-start | bytes 196616 | tf_op jit(solution)/shard_map/ppermute | solution.py:14
  7.8 4.0 %collective-permute-done = f32[2,64,1,128]{3,1,2,0:T(8,128)S(1)} collective-permute-done((f32[2,64,1,128]{3,1,2,0:T(8,128)S(1)}, f32[2,64,1,128]{3,1,2,0:T(8,128)S(1)}, u32[]{:S(2)}, u32[]{:S(2)}) %collective-permute-start) | collective-permute-done | bytes 65568 | tf_op jit(solution)/shard_map/ppermute | solution.py:14
  13.4 1.3 collective-permute-start.3
  15.1 5.2 %collective-permute-start.2 = (f32[2,64,18,1]{1,0,3,2:T(2,128)S(1)}, f32[2,64,18,1]{1,0,3,2:T(2,128)}, u32[]{:S(2)}, u32[]{:S(2)}) collective-permute-start(f32[2,64,18,1]{1,0,3,2:T(2,128)S(1)} %copy.267), channel_id=1, source_target_pairs={{0,1},{1,2},{2,3},{4,5},{5,6},{6,7},{8,9},{9,10},{10,11},{12,13},{... | collective-permute-start | bytes 27656 | tf_op jit(solution)/shard_map/ppermute | solution.py:14
  21.3 1.1 copy.269
  22.5 1.9 %pad_maximum_fusion = f32[2,64,18,130]{3,1,2,0:T(8,128)S(1)} fusion(f32[2,64,18,1]{3,1,2,0:T(8,128)S(1)} %copy.270, f32[2,64,1,128]{3,1,2,0:T(8,128)} %copy-done.14, f32[1,64,16,128]{3,1,2,0:T(8,128)S(1)} %get-tuple-element.1003, f32[1,64,16,128]{3,1,2,0:T(8,128)S(1)} %get-tuple-element.896, f32[2,64,1,128]{3,1,2,0:T(8,128)} %copy-done.15, ...), kind=kLoop, calls=%fused_computation.42 | loop fusion | flops 1497600 | bytes 2396160 | tf_op jit(solution)/shard_map/concatenate | solution.py:18
  24.5 0.8 copy-done
  25.7 1.1 subtract_subtract_fusion.1
  27.5 0.8 multiply_add_fusion.30
  29.5 1.1 multiply_add_fusion.37
  31.3 0.9 multiply_add_fusion.35
  32.6 0.7 multiply_add_fusion.33
  34.6 0.7 copy-done.1
  35.4 0.7 multiply_add_fusion.11
  36.1 4.5 %collective-permute-done.4 = f32[1,6,64,128]{3,2,1,0:T(8,128)S(1)} collective-permute-done((f32[1,6,64,128]{3,2,1,0:T(8,128)S(1)}, f32[1,6,64,128]{3,2,1,0:T(8,128)S(1)}, u32[]{:S(2)}, u32[]{:S(2)}) %collective-permute-start.4) | collective-permute-done | bytes 196640 | tf_op jit(solution)/shard_map/ppermute | solution.py:154
  40.5 0.9 fusion.100
  41.5 5.0 %collective-permute-done.5 = f32[1,6,64,128]{3,2,1,0:T(8,128)S(1)} collective-permute-done((f32[1,6,64,128]{3,2,1,0:T(8,128)S(1)}, f32[1,6,64,128]{3,2,1,0:T(8,128)S(1)}, u32[]{:S(2)}, u32[]{:S(2)}) %collective-permute-start.5) | collective-permute-done | bytes 196640 | tf_op jit(solution)/shard_map/ppermute | solution.py:154
  46.5 1.0 fusion.98
  47.6 5.0 %collective-permute-done.6 = f32[1,6,64,128]{3,2,1,0:T(8,128)S(1)} collective-permute-done((f32[1,6,64,128]{3,2,1,0:T(8,128)S(1)}, f32[1,6,64,128]{3,2,1,0:T(8,128)S(1)}, u32[]{:S(2)}, u32[]{:S(2)}) %collective-permute-start.6) | collective-permute-done | bytes 196640 | tf_op jit(solution)/shard_map/ppermute | solution.py:154
  52.8 5.7 %collective-permute-done.7 = f32[1,6,64,128]{3,2,1,0:T(8,128)S(1)} collective-permute-done((f32[1,6,64,128]{3,2,1,0:T(8,128)S(1)}, f32[1,6,64,128]{3,2,1,0:T(8,128)S(1)}, u32[]{:S(2)}, u32[]{:S(2)}) %collective-permute-start.7) | collective-permute-done | bytes 196640 | tf_op jit(solution)/shard_map/ppermute | solution.py:154
  58.5 1.1 fusion.81
  59.7 4.9 %collective-permute-done.8 = f32[1,6,64,128]{3,2,1,0:T(8,128)S(1)} collective-permute-done((f32[1,6,64,128]{3,2,1,0:T(8,128)S(1)}, f32[1,6,64,128]{3,2,1,0:T(8,128)S(1)}, u32[]{:S(2)}, u32[]{:S(2)}) %collective-permute-start.8) | collective-permute-done | bytes 196640 | tf_op jit(solution)/shard_map/ppermute | solution.py:154
  64.5 1.2 fusion.101
  65.7 4.8 %collective-permute-done.9 = f32[1,6,64,128]{3,2,1,0:T(8,128)S(1)} collective-permute-done((f32[1,6,64,128]{3,2,1,0:T(8,128)S(1)}, f32[1,6,64,128]{3,2,1,0:T(8,128)S(1)}, u32[]{:S(2)}, u32[]{:S(2)}) %collective-permute-start.9) | collective-permute-done | bytes 196640 | tf_op jit(solution)/shard_map/ppermute | solution.py:154
  70.5 1.1 fusion.99
  71.7 4.8 %collective-permute-done.10 = f32[1,6,64,128]{3,2,1,0:T(8,128)S(1)} collective-permute-done((f32[1,6,64,128]{3,2,1,0:T(8,128)S(1)}, f32[1,6,64,128]{3,2,1,0:T(8,128)S(1)}, u32[]{:S(2)}, u32[]{:S(2)}) %collective-permute-start.10) | collective-permute-done | bytes 196640 | tf_op jit(solution)/shard_map/ppermute | solution.py:154
  76.9 1.1 dynamic-slice_bitcast_fusion
  78.0 0.7 broadcast.345.clone.1
  78.7 0.7 broadcast.345.clone.2
  79.4 0.8 broadcast.345.clone.3
  80.2 0.7 broadcast.345.clone.4
  80.9 12.0 %while.80 = (s32[]{:T(128)}, f32[64,128]{1,0:T(8,128)S(1)}, f32[64,128]{1,0:T(8,128)S(1)}, f32[8,64,128]{2,1,0:T(8,128)}, f32[8,64,128]{2,1,0:T(8,128)}, /*index...) while((s32[]{:T(128)}, f32[64,128]{1,0:T(8,128)S(1)}, ...), condition=%wide.region_1.2_spmd.clone, body=%wide.region_0.1_spmd.clone.sunk | while | flops 122883 | bytes 458915 | solution.py:103
  80.9 1.5 %bitcast_dynamic-update-slice_fusion.16 = (f32[8,64,128]{2,1,0:T(8,128)}, f32[64,128]{1,0:T(8,128)S(1)}, f32[8,64,128]{2,1,0:T(8,128)}, f32[8,64,128]{2,1,0:T(8,...) fusion(f32[8,64,128]{2,1,0:T(8,128)} %get-tuple-element.1322, s32[]{:T(128)S(6)} %copy.375, ...), kind=kLoop, calls=%fused_computation.clone.1 | loop fusion | flops 122880 | bytes 458757 | tf_op jit(solution)/shard_map/while/body/jit(dynamic_update_index_in_dim)/dynamic_update_slice | solution.py:103
  82.4 1.5 %bitcast_dynamic-update-slice_fusion.16 = (f32[8,64,128]{2,1,0:T(8,128)}, f32[64,128]{1,0:T(8,128)S(1)}, f32[8,64,128]{2,1,0:T(8,128)}, f32[8,64,128]{2,1,0:T(8,...) fusion(f32[8,64,128]{2,1,0:T(8,128)} %get-tuple-element.1322, s32[]{:T(128)S(6)} %copy.375, ...), kind=kLoop, calls=%fused_computation.clone.1 | loop fusion | flops 122880 | bytes 458757 | tf_op jit(solution)/shard_map/while/body/jit(dynamic_update_index_in_dim)/dynamic_update_slice | solution.py:103
  83.9 1.5 %bitcast_dynamic-update-slice_fusion.16 = (f32[8,64,128]{2,1,0:T(8,128)}, f32[64,128]{1,0:T(8,128)S(1)}, f32[8,64,128]{2,1,0:T(8,128)}, f32[8,64,128]{2,1,0:T(8,...) fusion(f32[8,64,128]{2,1,0:T(8,128)} %get-tuple-element.1322, s32[]{:T(128)S(6)} %copy.375, ...), kind=kLoop, calls=%fused_computation.clone.1 | loop fusion | flops 122880 | bytes 458757 | tf_op jit(solution)/shard_map/while/body/jit(dynamic_update_index_in_dim)/dynamic_update_slice | solution.py:103
  85.4 1.5 %bitcast_dynamic-update-slice_fusion.16 = (f32[8,64,128]{2,1,0:T(8,128)}, f32[64,128]{1,0:T(8,128)S(1)}, f32[8,64,128]{2,1,0:T(8,128)}, f32[8,64,128]{2,1,0:T(8,...) fusion(f32[8,64,128]{2,1,0:T(8,128)} %get-tuple-element.1322, s32[]{:T(128)S(6)} %copy.375, ...), kind=kLoop, calls=%fused_computation.clone.1 | loop fusion | flops 122880 | bytes 458757 | tf_op jit(solution)/shard_map/while/body/jit(dynamic_update_index_in_dim)/dynamic_update_slice | solution.py:103
  86.9 1.5 %bitcast_dynamic-update-slice_fusion.16 = (f32[8,64,128]{2,1,0:T(8,128)}, f32[64,128]{1,0:T(8,128)S(1)}, f32[8,64,128]{2,1,0:T(8,128)}, f32[8,64,128]{2,1,0:T(8,...) fusion(f32[8,64,128]{2,1,0:T(8,128)} %get-tuple-element.1322, s32[]{:T(128)S(6)} %copy.375, ...), kind=kLoop, calls=%fused_computation.clone.1 | loop fusion | flops 122880 | bytes 458757 | tf_op jit(solution)/shard_map/while/body/jit(dynamic_update_index_in_dim)/dynamic_update_slice | solution.py:103
  88.4 1.5 %bitcast_dynamic-update-slice_fusion.16 = (f32[8,64,128]{2,1,0:T(8,128)}, f32[64,128]{1,0:T(8,128)S(1)}, f32[8,64,128]{2,1,0:T(8,128)}, f32[8,64,128]{2,1,0:T(8,...) fusion(f32[8,64,128]{2,1,0:T(8,128)} %get-tuple-element.1322, s32[]{:T(128)S(6)} %copy.375, ...), kind=kLoop, calls=%fused_computation.clone.1 | loop fusion | flops 122880 | bytes 458757 | tf_op jit(solution)/shard_map/while/body/jit(dynamic_update_index_in_dim)/dynamic_update_slice | solution.py:103
  89.9 1.5 %bitcast_dynamic-update-slice_fusion.16 = (f32[8,64,128]{2,1,0:T(8,128)}, f32[64,128]{1,0:T(8,128)S(1)}, f32[8,64,128]{2,1,0:T(8,128)}, f32[8,64,128]{2,1,0:T(8,...) fusion(f32[8,64,128]{2,1,0:T(8,128)} %get-tuple-element.1322, s32[]{:T(128)S(6)} %copy.375, ...), kind=kLoop, calls=%fused_computation.clone.1 | loop fusion | flops 122880 | bytes 458757 | tf_op jit(solution)/shard_map/while/body/jit(dynamic_update_index_in_dim)/dynamic_update_slice | solution.py:103
  91.4 1.5 %bitcast_dynamic-update-slice_fusion.16 = (f32[8,64,128]{2,1,0:T(8,128)}, f32[64,128]{1,0:T(8,128)S(1)}, f32[8,64,128]{2,1,0:T(8,128)}, f32[8,64,128]{2,1,0:T(8,...) fusion(f32[8,64,128]{2,1,0:T(8,128)} %get-tuple-element.1322, s32[]{:T(128)S(6)} %copy.375, ...), kind=kLoop, calls=%fused_computation.clone.1 | loop fusion | flops 122880 | bytes 458757 | tf_op jit(solution)/shard_map/while/body/jit(dynamic_update_index_in_dim)/dynamic_update_slice | solution.py:103
  92.9 0.7 broadcast.345.clone
  93.7 11.4 %while.81 = (s32[]{:T(128)}, f32[64,128]{1,0:T(8,128)S(1)}, f32[8,64,128]{2,1,0:T(8,128)S(1)}, f32[8,64,128]{2,1,0:T(8,128)}, f32[8,64,128]{2,1,0:T(8,128)}, /*i...) while((s32[]{:T(128)}, f32[64,128]{1,0:T(8,128)S(1)}, ...), condition=%wide.region_3.4_spmd.clone, body=%wide.region_2.3_spmd.clone.sunk | while | flops 40964 | bytes 262287 | solution.py:111
  93.7 1.4 %bitcast_dynamic-update-slice_fusion.17 = (f32[8,64,128]{2,1,0:T(8,128)S(1)}, f32[64,128]{1,0:T(8,128)S(1)}, f32[8,64,128]{2,1,0:T(8,128)}) fusion(f32[8,64,128]{2,1,0:T(8,128)S(1)} %get-tuple-element.1359, s32[]{:T(128)S(6)} %sub.278, f32[64,128]{1,0:T(8,128)S(1)} %get-tuple-element.1358, pred[]{:T(512)S(6)} %compare.144, ...), kind=kLoop, calls=%fused_computation.18.clone.1 | loop fusion | flops 40960 | bytes 262149 | tf_op jit(solution)/shard_map/while/body/jit(dynamic_update_index_in_dim)/dynamic_update_slice | solution.py:103
  95.1 1.4 %bitcast_dynamic-update-slice_fusion.17 = (f32[8,64,128]{2,1,0:T(8,128)S(1)}, f32[64,128]{1,0:T(8,128)S(1)}, f32[8,64,128]{2,1,0:T(8,128)}) fusion(f32[8,64,128]{2,1,0:T(8,128)S(1)} %get-tuple-element.1359, s32[]{:T(128)S(6)} %sub.278, f32[64,128]{1,0:T(8,128)S(1)} %get-tuple-element.1358, pred[]{:T(512)S(6)} %compare.144, ...), kind=kLoop, calls=%fused_computation.18.clone.1 | loop fusion | flops 40960 | bytes 262149 | tf_op jit(solution)/shard_map/while/body/jit(dynamic_update_index_in_dim)/dynamic_update_slice | solution.py:103
  96.5 1.4 %bitcast_dynamic-update-slice_fusion.17 = (f32[8,64,128]{2,1,0:T(8,128)S(1)}, f32[64,128]{1,0:T(8,128)S(1)}, f32[8,64,128]{2,1,0:T(8,128)}) fusion(f32[8,64,128]{2,1,0:T(8,128)S(1)} %get-tuple-element.1359, s32[]{:T(128)S(6)} %sub.278, f32[64,128]{1,0:T(8,128)S(1)} %get-tuple-element.1358, pred[]{:T(512)S(6)} %compare.144, ...), kind=kLoop, calls=%fused_computation.18.clone.1 | loop fusion | flops 40960 | bytes 262149 | tf_op jit(solution)/shard_map/while/body/jit(dynamic_update_index_in_dim)/dynamic_update_slice | solution.py:103
  98.0 1.4 %bitcast_dynamic-update-slice_fusion.17 = (f32[8,64,128]{2,1,0:T(8,128)S(1)}, f32[64,128]{1,0:T(8,128)S(1)}, f32[8,64,128]{2,1,0:T(8,128)}) fusion(f32[8,64,128]{2,1,0:T(8,128)S(1)} %get-tuple-element.1359, s32[]{:T(128)S(6)} %sub.278, f32[64,128]{1,0:T(8,128)S(1)} %get-tuple-element.1358, pred[]{:T(512)S(6)} %compare.144, ...), kind=kLoop, calls=%fused_computation.18.clone.1 | loop fusion | flops 40960 | bytes 262149 | tf_op jit(solution)/shard_map/while/body/jit(dynamic_update_index_in_dim)/dynamic_update_slice | solution.py:103
  99.4 1.4 %bitcast_dynamic-update-slice_fusion.17 = (f32[8,64,128]{2,1,0:T(8,128)S(1)}, f32[64,128]{1,0:T(8,128)S(1)}, f32[8,64,128]{2,1,0:T(8,128)}) fusion(f32[8,64,128]{2,1,0:T(8,128)S(1)} %get-tuple-element.1359, s32[]{:T(128)S(6)} %sub.278, f32[64,128]{1,0:T(8,128)S(1)} %get-tuple-element.1358, pred[]{:T(512)S(6)} %compare.144, ...), kind=kLoop, calls=%fused_computation.18.clone.1 | loop fusion | flops 40960 | bytes 262149 | tf_op jit(solution)/shard_map/while/body/jit(dynamic_update_index_in_dim)/dynamic_update_slice | solution.py:103
  100.8 1.4 %bitcast_dynamic-update-slice_fusion.17 = (f32[8,64,128]{2,1,0:T(8,128)S(1)}, f32[64,128]{1,0:T(8,128)S(1)}, f32[8,64,128]{2,1,0:T(8,128)}) fusion(f32[8,64,128]{2,1,0:T(8,128)S(1)} %get-tuple-element.1359, s32[]{:T(128)S(6)} %sub.278, f32[64,128]{1,0:T(8,128)S(1)} %get-tuple-element.1358, pred[]{:T(512)S(6)} %compare.144, ...), kind=kLoop, calls=%fused_computation.18.clone.1 | loop fusion | flops 40960 | bytes 262149 | tf_op jit(solution)/shard_map/while/body/jit(dynamic_update_index_in_dim)/dynamic_update_slice | solution.py:103
  102.2 1.4 %bitcast_dynamic-update-slice_fusion.17 = (f32[8,64,128]{2,1,0:T(8,128)S(1)}, f32[64,128]{1,0:T(8,128)S(1)}, f32[8,64,128]{2,1,0:T(8,128)}) fusion(f32[8,64,128]{2,1,0:T(8,128)S(1)} %get-tuple-element.1359, s32[]{:T(128)S(6)} %sub.278, f32[64,128]{1,0:T(8,128)S(1)} %get-tuple-element.1358, pred[]{:T(512)S(6)} %compare.144, ...), kind=kLoop, calls=%fused_computation.18.clone.1 | loop fusion | flops 40960 | bytes 262149 | tf_op jit(solution)/shard_map/while/body/jit(dynamic_update_index_in_dim)/dynamic_update_slice | solution.py:103
  103.7 1.4 %bitcast_dynamic-update-slice_fusion.17 = (f32[8,64,128]{2,1,0:T(8,128)S(1)}, f32[64,128]{1,0:T(8,128)S(1)}, f32[8,64,128]{2,1,0:T(8,128)}) fusion(f32[8,64,128]{2,1,0:T(8,128)S(1)} %get-tuple-element.1359, s32[]{:T(128)S(6)} %sub.278, f32[64,128]{1,0:T(8,128)S(1)} %get-tuple-element.1358, pred[]{:T(512)S(6)} %compare.144, ...), kind=kLoop, calls=%fused_computation.18.clone.1 | loop fusion | flops 40960 | bytes 262149 | tf_op jit(solution)/shard_map/while/body/jit(dynamic_update_index_in_dim)/dynamic_update_slice | solution.py:103
  105.2 0.9 multiply_bitcast_fusion.1
  106.1 1.6 %multiply_subtract_fusion = f32[64,16,128]{2,0,1:T(8,128)S(1)} fusion(f32[64,16,128]{2,0,1:T(8,128)} %copy-done.2, f32[64,16,128]{2,0,1:T(8,128)S(1)} %add_divide_fusion.5, f32[64,16,128]{2,0,1:T(8,128)} %copy-done.1, f32[64,128]{1,0:T(8,128)S(1)} %multiply_bitcast_fusion, f32[64,128]{1,0:T(8,128)S(1)} %multiply_bitcast_fusion.1), kind=kLoop, calls=%fused_computation.145 | loop fusion | flops 524288 | bytes 2162688 | tf_op jit(solution)/shard_map/sub | solution.py:120
  108.0 0.9 multiply_add_fusion.24
  110.4 1.0 multiply_add_fusion.22
  113.0 1.0 multiply_add_fusion.20
  115.6 1.0 multiply_add_fusion.18
  118.2 1.0 multiply_add_fusion.16
  120.2 0.7 multiply_add_fusion.14
  121.7 0.8 add_divide_fusion.2
  123.1 0.8 add_divide_fusion.1
  125.0 14.8 %all-gather = f32[24,64,16]{1,2,0:T(8,128)S(1)} all-gather(f32[6,64,16]{1,2,0:T(8,128)S(1)} %constant_dynamic-update-slice_fusion.22), channel_id=2, replica_groups=mesh['row'=8,'col'=4] {'col'}, dimensions={0}, use_global_device_ids=true | all-gather | bytes 122880 | tf_op jit(solution)/shard_map/all_gather | solution.py:170
  140.7 1.1 copy.292
  (183 shorter events, 19.7 us)
Async XLA Ops:
  2.5 5.3 %collective-permute-start.1 = (f32[2,64,1,128]{3,1,2,0:T(8,128)S(1)}, f32[2,64,1,128]{3,1,2,0:T(8,128)S(1)}, u32[]{:S(2)}, u32[]{:S(2)}) collective-permute-start(f32[2,64,1,128]{3,1,2,0:T(8,128)S(1)} %get-tuple-element.864), channel_id=1, source_target_pairs={{4,0},{8,4},{12,8},{16,12},{20,16},{24,20},{28,24},{5,1},{9,5},{13... | collective-permute-start | bytes 196616 | tf_op jit(solution)/shard_map/ppermute | solution.py:17
  5.3 6.5 %collective-permute-start = (f32[2,64,1,128]{3,1,2,0:T(8,128)S(1)}, f32[2,64,1,128]{3,1,2,0:T(8,128)S(1)}, u32[]{:S(2)}, u32[]{:S(2)}) collective-permute-start(f32[2,64,1,128]{3,1,2,0:T(8,128)S(1)} %get-tuple-element.863), channel_id=1, source_target_pairs={{0,4},{4,8},{8,12},{12,16},{16,20},{20,24},{24,28},{1,5},{5,9},{9,... | collective-permute-start | bytes 196616 | tf_op jit(solution)/shard_map/ppermute | solution.py:14
  7.8 4.0 %copy-start.14 = (f32[2,64,1,128]{3,1,2,0:T(8,128)}, f32[2,64,1,128]{3,1,2,0:T(8,128)S(1)}, u32[]{:S(2)}) copy-start(f32[2,64,1,128]{3,1,2,0:T(8,128)S(1)} %collective-permute-done.1) | copy-start | bytes 196612
  11.8 0.6 copy-start.15
  13.4 7.4 %collective-permute-start.3 = (f32[2,64,18,1]{1,0,3,2:T(2,128)S(1)}, f32[2,64,18,1]{1,0,3,2:T(2,128)S(1)}, u32[]{:S(2)}, u32[]{:S(2)}) collective-permute-start(f32[2,64,18,1]{1,0,3,2:T(2,128)S(1)} %copy.268), channel_id=1, source_target_pairs={{1,0},{2,1},{3,2},{5,4},{6,5},{7,6},{9,8},{10,9},{11,10},{13,12},{... | collective-permute-start | bytes 27656 | tf_op jit(solution)/shard_map/ppermute | solution.py:17
  15.1 6.2 %collective-permute-start.2 = (f32[2,64,18,1]{1,0,3,2:T(2,128)S(1)}, f32[2,64,18,1]{1,0,3,2:T(2,128)}, u32[]{:S(2)}, u32[]{:S(2)}) collective-permute-start(f32[2,64,18,1]{1,0,3,2:T(2,128)S(1)} %copy.267), channel_id=1, source_target_pairs={{0,1},{1,2},{2,3},{4,5},{5,6},{6,7},{8,9},{9,10},{10,11},{12,13},{... | collective-permute-start | bytes 27656 | tf_op jit(solution)/shard_map/ppermute | solution.py:14
  24.3 1.0 copy-start
  24.3 1.2 copy-start.12
  24.3 1.3 copy-start.13
  24.4 1.3 copy-start.16
  26.8 0.7 copy-start.18
  33.8 1.5 %copy-start.17 = (pred[128]{0:T(512)(128)(4,1)S(1)}, pred[128]{0:T(512)(128)(4,1)}, u32[]{:S(2)}) copy-start(pred[128]{0:T(512)(128)(4,1)} %get-tuple-element.1007) | copy-start | bytes 388
  34.4 0.8 copy-start.1
  34.4 1.0 copy-start.2
  34.5 6.0 %collective-permute-start.4 = (f32[1,6,64,128]{3,2,1,0:T(8,128)S(1)}, f32[1,6,64,128]{3,2,1,0:T(8,128)S(1)}, u32[]{:S(2)}, u32[]{:S(2)}) collective-permute-start(f32[1,6,64,128]{3,2,1,0:T(8,128)S(1)} %bitcast.271), channel_id=1, source_target_pairs={{0,4},{4,8},{8,12},{12,16},{16,20},{20,24},{24,28},{28,0},{1,5},{5... | collective-permute-start | bytes 589832 | tf_op jit(solution)/shard_map/ppermute | solution.py:154
  40.5 6.0 %collective-permute-start.5 = (f32[1,6,64,128]{3,2,1,0:T(8,128)S(1)}, f32[1,6,64,128]{3,2,1,0:T(8,128)S(1)}, u32[]{:S(2)}, u32[]{:S(2)}) collective-permute-start(f32[1,6,64,128]{3,2,1,0:T(8,128)S(1)} %collective-permute-done.4), channel_id=1, source_target_pairs={{0,4},{4,8},{8,12},{12,16},{16,20},{20,24},{24,28},{28,0},{1,5},{5... | collective-permute-start | bytes 589832 | tf_op jit(solution)/shard_map/ppermute | solution.py:154
  46.5 6.0 %collective-permute-start.6 = (f32[1,6,64,128]{3,2,1,0:T(8,128)S(1)}, f32[1,6,64,128]{3,2,1,0:T(8,128)S(1)}, u32[]{:S(2)}, u32[]{:S(2)}) collective-permute-start(f32[1,6,64,128]{3,2,1,0:T(8,128)S(1)} %collective-permute-done.5), channel_id=1, source_target_pairs={{0,4},{4,8},{8,12},{12,16},{16,20},{20,24},{24,28},{28,0},{1,5},{5... | collective-permute-start | bytes 589832 | tf_op jit(solution)/shard_map/ppermute | solution.py:154
  52.5 6.0 %collective-permute-start.7 = (f32[1,6,64,128]{3,2,1,0:T(8,128)S(1)}, f32[1,6,64,128]{3,2,1,0:T(8,128)S(1)}, u32[]{:S(2)}, u32[]{:S(2)}) collective-permute-start(f32[1,6,64,128]{3,2,1,0:T(8,128)S(1)} %collective-permute-done.6), channel_id=1, source_target_pairs={{0,4},{4,8},{8,12},{12,16},{16,20},{20,24},{24,28},{28,0},{1,5},{5... | collective-permute-start | bytes 589832 | tf_op jit(solution)/shard_map/ppermute | solution.py:154
  58.5 6.0 %collective-permute-start.8 = (f32[1,6,64,128]{3,2,1,0:T(8,128)S(1)}, f32[1,6,64,128]{3,2,1,0:T(8,128)S(1)}, u32[]{:S(2)}, u32[]{:S(2)}) collective-permute-start(f32[1,6,64,128]{3,2,1,0:T(8,128)S(1)} %collective-permute-done.7), channel_id=1, source_target_pairs={{0,4},{4,8},{8,12},{12,16},{16,20},{20,24},{24,28},{28,0},{1,5},{5... | collective-permute-start | bytes 589832 | tf_op jit(solution)/shard_map/ppermute | solution.py:154
  64.5 6.0 %collective-permute-start.9 = (f32[1,6,64,128]{3,2,1,0:T(8,128)S(1)}, f32[1,6,64,128]{3,2,1,0:T(8,128)S(1)}, u32[]{:S(2)}, u32[]{:S(2)}) collective-permute-start(f32[1,6,64,128]{3,2,1,0:T(8,128)S(1)} %collective-permute-done.8), channel_id=1, source_target_pairs={{0,4},{4,8},{8,12},{12,16},{16,20},{20,24},{24,28},{28,0},{1,5},{5... | collective-permute-start | bytes 589832 | tf_op jit(solution)/shard_map/ppermute | solution.py:154
  70.5 6.0 %collective-permute-start.10 = (f32[1,6,64,128]{3,2,1,0:T(8,128)S(1)}, f32[1,6,64,128]{3,2,1,0:T(8,128)S(1)}, u32[]{:S(2)}, u32[]{:S(2)}) collective-permute-start(f32[1,6,64,128]{3,2,1,0:T(8,128)S(1)} %collective-permute-done.9), channel_id=1, source_target_pairs={{0,4},{4,8},{8,12},{12,16},{16,20},{20,24},{24,28},{28,0},{1,5},{5... | collective-permute-start | bytes 589832 | tf_op jit(solution)/shard_map/ppermute | solution.py:154
  105.1 2.8 %copy-start.4 = (f32[64,16,127]{2,0,1:T(8,128)S(1)}, f32[64,16,127]{2,0,1:T(8,128)}, u32[]{:S(2)}) copy-start(f32[64,16,127]{2,0,1:T(8,128)} %get-tuple-element.989) | copy-start | bytes 1560580
  105.1 2.8 %copy-start.5 = (f32[64,16,127]{2,0,1:T(8,128)S(1)}, f32[64,16,127]{2,0,1:T(8,128)}, u32[]{:S(2)}) copy-start(f32[64,16,127]{2,0,1:T(8,128)} %get-tuple-element.985) | copy-start | bytes 1560580
  105.1 2.8 %copy-start.6 = (f32[64,16,127]{2,0,1:T(8,128)S(1)}, f32[64,16,127]{2,0,1:T(8,128)}, u32[]{:S(2)}) copy-start(f32[64,16,127]{2,0,1:T(8,128)} %get-tuple-element.951) | copy-start | bytes 1560580
  105.1 2.8 %copy-start.7 = (f32[64,16,127]{2,0,1:T(8,128)S(1)}, f32[64,16,127]{2,0,1:T(8,128)}, u32[]{:S(2)}) copy-start(f32[64,16,127]{2,0,1:T(8,128)} %get-tuple-element.952) | copy-start | bytes 1560580
  105.1 2.8 %copy-start.8 = (f32[64,16,126]{2,0,1:T(8,128)S(1)}, f32[64,16,126]{2,0,1:T(8,128)}, u32[]{:S(2)}) copy-start(f32[64,16,126]{2,0,1:T(8,128)} %get-tuple-element.991) | copy-start | bytes 1548292
  105.1 2.8 %copy-start.9 = (f32[64,16,126]{2,0,1:T(8,128)S(1)}, f32[64,16,126]{2,0,1:T(8,128)}, u32[]{:S(2)}) copy-start(f32[64,16,126]{2,0,1:T(8,128)} %get-tuple-element.992) | copy-start | bytes 1548292
  105.1 2.8 %copy-start.10 = (f32[64,16,126]{2,0,1:T(8,128)S(1)}, f32[64,16,126]{2,0,1:T(8,128)}, u32[]{:S(2)}) copy-start(f32[64,16,126]{2,0,1:T(8,128)} %get-tuple-element.987) | copy-start | bytes 1548292
  105.1 2.8 %copy-start.11 = (f32[64,16,126]{2,0,1:T(8,128)S(1)}, f32[64,16,126]{2,0,1:T(8,128)}, u32[]{:S(2)}) copy-start(f32[64,16,126]{2,0,1:T(8,128)} %get-tuple-element.988) | copy-start | bytes 1548292
  123.9 16.4 %copy-start.3 = (f32[64,16,128]{2,1,0:T(8,128)S(1)}, f32[64,16,128]{2,1,0:T(8,128)}, u32[]{:S(2)}) copy-start(f32[64,16,128]{2,1,0:T(8,128)} %param.10) | copy-start | bytes 1572868
